TPU v7x, 32 devices: a whole 2x2x4 slice. The times are simulated.
32 devices in a mesh: row: 8 (over y, x, core), col: 4 (over z).
Axes of the slice: x: 2, y: 2, z: 4, core: 2. Of those that a mesh axis runs over, the one named last changes fastest.
Arguments:
- alignment_state: bfloat16 [128, 128, 256], P('col', 'row'), may hold values from -6 to 6
- layer_norm_gain: float32 [256], replicated, may hold values from 0.1 to 1.9
- left_weight_matrix: bfloat16 [256, 32], replicated, may hold values from -0.375 to 0.375
- right_weight_matrix: bfloat16 [256, 32], replicated, may hold values from -0.375 to 0.375
- output_weight_matrix: bfloat16 [1024, 128], replicated, may hold values from -0.1875 to 0.1875
- output_bias_vector: float32 [128], replicated, may hold values from -3 to 3
- pair_update_cotangent: bfloat16 [128, 128, 128], P('row', 'col'), may hold values from -40 to 40
Outputs:
- pair_update_output: bfloat16 [128, 128, 128], P('row', 'col')
- alignment_gradient: bfloat16 [128, 128, 256], P('col', 'row')
- left_weight_gradient: float32 [256, 32], replicated
- right_weight_gradient: float32 [256, 32], replicated
- out_w_grad: float32 [1024, 128], P(('row', 'col'))
- norm_gain_gradient: float32 [256], replicated
- output_bias_gradient: float32 [128], replicated
All inputs are finite; a program needn't handle non-finite values.
Results may differ from a plain program's by a relative error of at most 0.024.
Values may be sent and summed in bfloat16 or wider, within the bound.
No kernel may reach another device: no remote copies, remote signals or barrier semaphores. Data moves between devices by JAX's collectives and lax.ppermute only.
A program may use at most 64 MiB of HBM per device.

v0:
```python
import jax
import jax.numpy as jnp
from jax import lax
from jax.sharding import PartitionSpec as P


def from_root(block, axis, holder):
    block = jnp.where(lax.axis_index(axis) == holder, block, jnp.zeros_like(block))
    return lax.psum(block, axis)


def apply_layer_norm(alignment_state):
    value_entries = alignment_state.astype(jnp.float32)
    center = value_entries - jnp.mean(value_entries, axis=-1, keepdims=True)
    inverse_deviation = lax.rsqrt(jnp.mean(center * center, axis=-1, keepdims=True) + 1e-05)
    return (center * inverse_deviation, inverse_deviation)


def on_device(
    alignment_state,
    layer_norm_gain,
    left_weight_matrix,
    right_weight_matrix,
    output_weight_matrix,
    output_bias_vector,
    pair_update_cotangent,
):
    sequence_block_local, residue_block_local, alignment_weight = alignment_state.shape
    proj_w = left_weight_matrix.shape[1]
    pair_w = output_weight_matrix.shape[1]
    row_count = lax.axis_size("row")
    col_count = lax.axis_size("col")
    row_ratio = row_count // col_count
    total_res = residue_block_local * row_count
    col_res = residue_block_local * row_ratio
    col_index = lax.axis_index("col")
    row_index = lax.axis_index("row")
    normed_alignment, inverse_deviation = apply_layer_norm(alignment_state)
    layer_norm_output = (normed_alignment * layer_norm_gain).astype(jnp.bfloat16)
    normed_flat_rows = layer_norm_output.reshape(-1, alignment_weight)
    left_local = (
        jnp.dot(normed_flat_rows, left_weight_matrix, preferred_element_type=jnp.float32)
        .astype(jnp.bfloat16)
        .reshape(sequence_block_local, residue_block_local, proj_w)
    )
    right_local = (
        jnp.dot(normed_flat_rows, right_weight_matrix, preferred_element_type=jnp.float32)
        .astype(jnp.bfloat16)
        .reshape(sequence_block_local, residue_block_local, proj_w)
    )
    left_all, right_rows = (
        lax.all_gather(left_local, "col", axis=0, tiled=True),
        lax.all_gather(right_local, "col", axis=0, tiled=True),
    )
    seq_total = left_all.shape[0]
    right_every = lax.all_gather(right_rows, "row", axis=1, tiled=True)
    right_block = lax.dynamic_slice_in_dim(right_every, col_index * col_res, col_res, 1)
    block_res = min(8, residue_block_local)

    def visit(totals, row_start):
        right_acc, projection_running_sum = totals
        left_part = lax.dynamic_slice_in_dim(left_all, row_start, block_res, 1)
        cot_part = lax.dynamic_slice_in_dim(pair_update_cotangent, row_start, block_res, 0)
        outer_prod = jnp.einsum(
            "sic,sjd->ijcd", left_part, right_block, preferred_element_type=jnp.float32
        )
        outer_flat = (
            (outer_prod / seq_total)
            .astype(jnp.bfloat16)
            .reshape(block_res * col_res, proj_w * proj_w)
        )
        cot_flat = cot_part.reshape(block_res * col_res, pair_w)
        pair_part = (
            jnp.dot(outer_flat, output_weight_matrix, preferred_element_type=jnp.float32)
            + output_bias_vector
        ).astype(jnp.bfloat16)
        projection_running_sum = projection_running_sum + lax.dot_general(
            outer_flat, cot_flat, (((0,), (0,)), ((), ())), preferred_element_type=jnp.float32
        )
        outer_grad = lax.dot_general(
            cot_flat,
            output_weight_matrix,
            (((1,), (1,)), ((), ())),
            preferred_element_type=jnp.float32,
        ).astype(jnp.bfloat16)
        outer_grad = outer_grad.reshape(block_res, col_res, proj_w, proj_w)
        left_part_grad = (
            jnp.einsum("ijcd,sjd->sic", outer_grad, right_block, preferred_element_type=jnp.float32)
            / seq_total
        )
        right_acc = (
            right_acc
            + jnp.einsum("ijcd,sic->sjd", outer_grad, left_part, preferred_element_type=jnp.float32)
            / seq_total
        )
        return (
            (right_acc, projection_running_sum),
            (pair_part.reshape(block_res, col_res, pair_w), left_part_grad),
        )

    starts = jnp.arange(residue_block_local // block_res, dtype=jnp.int32) * block_res
    initial = (
        jnp.zeros((seq_total, col_res, proj_w), jnp.float32),
        jnp.zeros((proj_w * proj_w, pair_w), jnp.float32),
    )
    (right_acc, projection_running_sum), (pair_parts, left_parts) = lax.scan(visit, initial, starts)
    pair_update_output = pair_parts.reshape(residue_block_local, col_res, pair_w)
    left_partial = jnp.transpose(left_parts, (1, 0, 2, 3)).reshape(
        seq_total, residue_block_local, proj_w
    )
    left_d = lax.psum_scatter(
        left_partial.astype(jnp.bfloat16), "col", scatter_dimension=0, tiled=True
    )
    right_full = lax.psum(right_acc.astype(jnp.bfloat16), "row").astype(jnp.float32)
    right_half = lax.dynamic_slice_in_dim(
        right_full, row_index % row_ratio * residue_block_local, residue_block_local, 1
    )
    right_home = from_root(right_half.astype(jnp.bfloat16), "col", row_index // row_ratio).astype(
        right_half.dtype
    )
    right_d = lax.dynamic_slice_in_dim(
        right_home, col_index * sequence_block_local, sequence_block_local, 0
    ).astype(jnp.bfloat16)
    left_flat = left_d.reshape(-1, proj_w)
    right_flat = right_d.reshape(-1, proj_w)
    normed_derivative = lax.dot_general(
        left_flat, left_weight_matrix, (((1,), (1,)), ((), ())), preferred_element_type=jnp.float32
    )
    normed_derivative = normed_derivative + lax.dot_general(
        right_flat,
        right_weight_matrix,
        (((1,), (1,)), ((), ())),
        preferred_element_type=jnp.float32,
    )
    normed_derivative = normed_derivative.reshape(
        sequence_block_local, residue_block_local, alignment_weight
    )
    scaled_product = normed_derivative * layer_norm_gain
    alignment_gradient = (
        (
            scaled_product
            - jnp.mean(scaled_product, axis=-1, keepdims=True)
            - normed_alignment * jnp.mean(scaled_product * normed_alignment, axis=-1, keepdims=True)
        )
        * inverse_deviation
    ).astype(jnp.bfloat16)
    weight_left = lax.dot_general(
        normed_flat_rows, left_flat, (((0,), (0,)), ((), ())), preferred_element_type=jnp.float32
    )
    weight_right = lax.dot_general(
        normed_flat_rows, right_flat, (((0,), (0,)), ((), ())), preferred_element_type=jnp.float32
    )
    gain_part = jnp.sum(normed_derivative * normed_alignment, axis=(0, 1))
    bias_part = jnp.sum(pair_update_cotangent, axis=(0, 1), dtype=jnp.float32)
    param_totals = lax.psum((weight_left, weight_right, gain_part, bias_part), ("row", "col"))
    proj_partial = lax.psum_scatter(
        projection_running_sum.astype(jnp.bfloat16), "row", scatter_dimension=0, tiled=True
    ).astype(jnp.float32)
    proj_total = lax.psum_scatter(proj_partial, "col", scatter_dimension=0, tiled=True)
    return (
        pair_update_output,
        alignment_gradient,
        param_totals[0] / total_res,
        param_totals[1] / total_res,
        proj_total / total_res,
        param_totals[2] / total_res,
        param_totals[3] / total_res,
    )


def solution(mesh):
    return jax.shard_map(
        on_device,
        mesh=mesh,
        in_specs=(P("col", "row", None), P(), P(), P(), P(), P(), P("row", "col", None)),
        out_specs=(
            P("row", "col", None),
            P("col", "row", None),
            P(),
            P(),
            P(("row", "col"), None),
            P(),
            P(),
        ),
        check_vma=False,
    )
```

profile of v0, /device:TPU:0, one launch (start us, length us, event | category | flops | bytes accessed | tf_op | source)
XLA Modules:
  0.0 416.1 jit_solution(7871246451103388164)
XLA Ops:
  11.1 18.0 %all_gather.10 = bf16[128,16,32]{2,1,0:T(8,128)(2,1)} all-gather(bf16[32,16,32]{2,1,0:T(8,128)(2,1)S(1)} %bitcast.126), channel_id=1, replica_groups=mesh['row'=8,'col'=4] {'col'}, dimensions={0}, use_global_device_ids=true | all-gather | bytes 163840 | tf_op jit(solution)/shard_map/all_gather | solution.py:53
  29.6 16.3 %all_gather.9 = bf16[128,16,32]{2,1,0:T(8,128)(2,1)S(1)} all-gather(bf16[32,16,32]{2,1,0:T(8,128)(2,1)S(1)} %bitcast.127), channel_id=1, replica_groups=mesh['row'=8,'col'=4] {'col'}, dimensions={0}, use_global_device_ids=true | all-gather | bytes 163840 | tf_op jit(solution)/shard_map/all_gather | solution.py:52
  46.8 21.7 %all-gather.2.cloned.1.call-done = bf16[128,128,32]{2,1,0:T(8,128)(2,1)} async-done(((bf16[128,16,32]{2,1,0:T(8,128)(2,1)}), bf16[128,128,32]{2,1,0:T(8,128)(2,1)}) %all-gather.2.cloned.1.call-update) | async-done | bytes 1048592 | tf_op jit(solution)/shard_map/all_gather | solution.py:56
  69.8 1.8 copy.44
  71.6 32.6 %while.17 = (s32[]{:T(128)}, f32[128,32,32]{0,2,1:T(8,128)}, f32[1024,128]{1,0:T(8,128)S(1)}, bf16[2,8,32,128]{3,2,1,0:T(8,128)(2,1)}, bf16[2,128,8,32]{1,3,2,0:...) while((s32[]{:T(128)}, f32[128,32,32]{0,2,1:T(8,128)}, ...), condition=%wide.region_3.4_spmd.clone, body=%wide.region_2.3_spmd.clone.sunk | while | flops 404193280 | bytes 15928666 | solution.py:106
  74.8 1.7 fusion.79
  76.5 2.2 reshape.95
  81.1 1.6 reshape.94
  85.3 2.1 fusion.81
  90.6 1.7 fusion.79
  92.2 2.2 reshape.95
  96.9 1.6 reshape.94
  98.5 2.6 fusion.78
  102.1 2.1 fusion.81
  104.3 1.8 convert_element_type.67
  106.2 2.1 copy.45
  109.0 51.2 %all-reduce.5.cloned.1.call-done = bf16[128,32,32]{0,2,1:T(8,128)(2,1)} async-done(((bf16[128,32,32]{0,2,1:T(8,128)(2,1)}), bf16[128,32,32]{0,2,1:T(8,128)(2,1)}) %all-reduce.5.cloned.1.call-update) | async-done | bytes 262160 | tf_op jit(solution)/shard_map/psum | solution.py:114
  160.2 1.6 fusion.28
  161.8 21.9 %reduce-scatter.4.cloned.1.call-done = bf16[32,16,32]{2,1,0:T(8,128)(2,1)} async-done(((bf16[128,16,32]{2,1,0:T(8,128)(2,1)}), bf16[32,16,32]{2,1,0:T(8,128)(2,1)}) %reduce-scatter.4.cloned.1.call-update) | async-done | bytes 32784 | tf_op jit(solution)/shard_map/reduce_scatter | solution.py:111
  184.8 1.7 convolution_bitcast_fusion.3
  186.5 32.9 %all-reduce.7.cloned.1.call-done = bf16[128,16,32]{0,2,1:T(8,128)(2,1)} async-done(((bf16[128,16,32]{0,2,1:T(8,128)(2,1)}), bf16[128,16,32]{0,2,1:T(8,128)(2,1)}) %all-reduce.7.cloned.1.call-update) | async-done | bytes 131088 | tf_op jit(solution)/shard_map/psum | solution.py:9
  224.5 122.1 %all-reduce.9.cloned.1.call-done = (f32[256,32]{0,1:T(8,128)}, f32[256,32]{0,1:T(8,128)}, f32[256]{0:T(256)}, f32[128]{0:T(128)}) async-done(((f32[256,32]{0,1:T(8,128)}, f32[256,32]{0,1:T(8,128)}, f32[256]{0:T(256)}, f32[128]{0:T(128)}), (f32[256,32]{0,1:T(8,128)}, f32[256,32]{0,1:T(8,128)}, f32[256]{0:T(256)}, f32[128]{0:T(128)})) %all-reduce.9.cloned.1.call-update) | async-done | bytes 67088 | tf_op jit(solution)/shard_map/psum | solution.py:155
  349.3 37.1 %reduce-scatter.6.cloned.1.call-done = bf16[128,128]{1,0:T(8,128)(2,1)} async-done(((bf16[1024,128]{1,0:T(8,128)(2,1)}), bf16[128,128]{1,0:T(8,128)(2,1)}) %reduce-scatter.6.cloned.1.call-update) | async-done | bytes 32784 | tf_op jit(solution)/shard_map/reduce_scatter | solution.py:156
  388.9 19.1 %reduce-scatter.8.cloned.1.call-done = f32[32,128]{1,0:T(8,128)} async-done(((f32[128,128]{1,0:T(8,128)}), f32[32,128]{1,0:T(8,128)}) %reduce-scatter.8.cloned.1.call-update) | async-done | bytes 16400 | tf_op jit(solution)/shard_map/reduce_scatter | solution.py:159
  (106 shorter events, 30.6 us)
Async XLA Ops:
  7.2 3.6 copy-start
  7.2 22.1 %copy-start.12 = (bf16[256,32]{0,1:T(8,128)(2,1)S(1)}, bf16[256,32]{0,1:T(8,128)(2,1)}, u32[]{:S(2)}) copy-start(bf16[256,32]{0,1:T(8,128)(2,1)} %param.11) | copy-start | bytes 49156
  7.2 61.3 %all-gather.2.cloned.1.call-start = ((), (), s32[]{:S(2)}) async-start(), calls=%async_computation.3 | async-start | bytes 4718592 | tf_op jit(solution)/shard_map/all_gather | solution.py:56
  8.3 2.4 copy-start.8
  10.8 18.8 %copy-start.5 = (bf16[32,16,256]{2,1,0:T(8,128)(2,1)}, bf16[32,16,256]{2,1,0:T(8,128)(2,1)S(1)}, u32[]{:S(2)}) copy-start(bf16[32,16,256]{2,1,0:T(8,128)(2,1)S(1)} %fusion.21) | copy-start | bytes 786436
  29.1 131.0 %all-reduce.5.cloned.1.call-start = ((), (), s32[]{:S(2)}) async-start(), calls=%async_computation.5 | async-start | bytes 524288 | tf_op jit(solution)/shard_map/psum | solution.py:114
  45.9 25.7 %copy-start.1 = (bf16[1024,128]{1,0:T(8,128)(2,1)S(1)}, bf16[1024,128]{1,0:T(8,128)(2,1)}, u32[]{:S(2)}) copy-start(bf16[1024,128]{1,0:T(8,128)(2,1)} %param.13) | copy-start | bytes 786436
  82.7 1.9 copy-start.16
  84.3 3.1 copy-start.3
  98.5 2.7 copy-start.15
  98.5 2.9 copy-start.16
  101.1 3.1 copy-start.3
  104.2 4.1 copy-start.7
  104.2 79.5 %copy-start.13 = (bf16[256,32]{0,1:T(8,128)(2,1)S(1)}, bf16[256,32]{0,1:T(8,128)(2,1)}, u32[]{:S(2)}) copy-start(bf16[256,32]{0,1:T(8,128)(2,1)} %param.11) | copy-start | bytes 49156
  104.2 80.6 %copy-start.6 = (bf16[32,16,256]{2,1,0:T(8,128)(2,1)S(1)}, bf16[32,16,256]{2,1,0:T(8,128)(2,1)}, u32[]{:S(2)}) copy-start(bf16[32,16,256]{2,1,0:T(8,128)(2,1)} %copy-done.5) | copy-start | bytes 786436
  106.1 115.3 %copy-start.14 = (f32[256]{0:T(256)S(1)}, f32[256]{0:T(256)}, u32[]{:S(2)}) copy-start(f32[256]{0:T(256)} %param.10) | copy-start | bytes 3076
  106.1 77.6 %reduce-scatter.4.cloned.1.call-start = ((), (), s32[]{:S(2)}) async-start(), calls=%async_computation.4 | async-start | bytes 655360 | tf_op jit(solution)/shard_map/reduce_scatter | solution.py:111
  108.3 113.5 %copy-start.4 = (bf16[32,16,256]{2,1,0:T(8,128)(2,1)S(1)}, bf16[32,16,256]{2,1,0:T(8,128)(2,1)}, u32[]{:S(2)}) copy-start(bf16[32,16,256]{2,1,0:T(8,128)(2,1)} %param.9) | copy-start | bytes 786436
  108.3 113.5 %copy-start.9 = (f32[32,16]{1,0:T(8,128)S(1)}, f32[32,16]{1,0:T(8,128)}, u32[]{:S(2)}) copy-start(f32[32,16]{1,0:T(8,128)} %copy-done.8) | copy-start | bytes 6148
  108.3 113.5 %copy-start.11 = (f32[32,16]{1,0:T(8,128)S(1)}, f32[32,16]{1,0:T(8,128)}, u32[]{:S(2)}) copy-start(f32[32,16]{1,0:T(8,128)} %copy-done.10) | copy-start | bytes 6148
  108.3 111.1 %all-reduce.7.cloned.1.call-start = ((), (), s32[]{:S(2)}) async-start(), calls=%async_computation.6 | async-start | bytes 262144 | tf_op jit(solution)/shard_map/psum | solution.py:9
  161.8 184.9 %all-reduce.9.cloned.1.call-start = ((), (), s32[]{:S(2)}) async-start(), calls=%async_computation.9 | async-start | bytes 134144 | tf_op jit(solution)/shard_map/psum | solution.py:155
  222.5 163.9 %reduce-scatter.6.cloned.1.call-start = ((), (), s32[]{:S(2)}) async-start(), calls=%async_computation.7 | async-start | bytes 294912 | tf_op jit(solution)/shard_map/reduce_scatter | solution.py:156
  223.3 184.6 %reduce-scatter.8.cloned.1.call-start = ((), (), s32[]{:S(2)}) async-start(), calls=%async_computation.8 | async-start | bytes 81920 | tf_op jit(solution)/shard_map/reduce_scatter | solution.py:159
  (6 other events, 5.7 us)
Sparse Core Ops, SparseCore 0:
  29.3 39.2 all-gather.1
  106.2 53.8 all-reduce.4
  162.4 21.2 reduce-scatter.3
  186.5 32.8 all-reduce.6
  225.9 120.6 all-reduce.8
  349.5 36.8 reduce-scatter.5
  388.6 19.2 reduce-scatter.7
where the time goes:
time: 417 us; the launch traced here: 416 us
  waiting for transfers between devices  306 us (73%)
  blocking collectives  34.3 us (8%)
  local copies, waits for them, and re-layouts  21 us (5%)
  matrix products  18.1 us (4%)
  other arithmetic  18 us (4%)
  between operations  14.4 us (3%)
    psum x1, waiting for transfers between devices, on_device(): lax.psum((weight_left, weight_right, gain_part, bias_part), ('row', 'col'))  122 us
    psum x1, waiting for transfers between devices, on_device(): lax.psum(right_acc.astype(jnp.bfloat16), 'row').astype(jnp.float32)  51.2 us
    reduce_scatter x1, waiting for transfers between devices, on_device(): lax.psum_scatter(projection_running_sum.astype(jnp.bfloat16), 'row', scat...  37.1 us
    psum x1, waiting for transfers between devices, from_root(): return lax.psum(block, axis)  32.9 us
    reduce_scatter x1, waiting for transfers between devices, on_device(): lax.psum_scatter(left_partial.astype(jnp.bfloat16), 'col', scatter_dimens...  21.9 us
    all_gather x1, waiting for transfers between devices, on_device(): right_every = lax.all_gather(right_rows, 'row', axis=1, tiled=True)  21.7 us
    reduce_scatter x1, waiting for transfers between devices, on_device(): lax.psum_scatter(proj_partial, 'col', scatter_dimension=0, tiled=True)  19.1 us
    all_gather x1, blocking collectives, on_device(): lax.all_gather(right_local, 'col', axis=0, tiled=True)  18 us
  transfers between devices with their start and end apart: 7, of which 7 were waited for; matrix products, arithmetic and copies ran while one was open for 3% of the time, Pallas kernels for 0%

commit v1 on v0

--- a/solution.py
+++ b/solution.py
@@ -3,10 +3,12 @@
 from jax import lax
 from jax.sharding import PartitionSpec as P
 
+_cut_runs = lambda inner_x, along_axis: lax.all_gather(inner_x, along_axis).sum(axis=0)
+
 
 def from_root(block, axis, holder):
     block = jnp.where(lax.axis_index(axis) == holder, block, jnp.zeros_like(block))
-    return lax.psum(block, axis)
+    return _cut_runs(block, axis)
 
 
 def apply_layer_norm(alignment_state):

time: 417 us -> 382 us (0.916)
  waiting for transfers between devices: 306 us -> 252 us
  blocking collectives: 34.3 us -> 54.1 us
    psum x1 -> x0, waiting for transfers between devices: 32.9 us -> none  [from_root(): return lax.psum(block, axis)]
    all_gather x0 -> x1, blocking collectives: none -> 19.8 us  [lax.all_gather(inner_x, along_axis).sum(axis=0)]
    reduce_scatter x1, waiting for transfers between devices: 21.9 us -> 2.88 us  [on_device(): lax.psum_scatter(left_partial.astype(jnp.bfloat16), 'col', scatter_dimens...]
  transfers between devices with their start and end apart: 7 -> 6, of which waited for: 7 -> 6; matrix products, arithmetic and copies ran while one was open for 3% -> 4% of each run, Pallas kernels for 0% -> 0%
where the time goes in v1:
time: 382 us; the launch traced here: 381 us
  waiting for transfers between devices  252 us (66%)
  blocking collectives  54.1 us (14%)
  local copies, waits for them, and re-layouts  21.1 us (6%)
  other arithmetic  18 us (5%)
  matrix products  17.3 us (5%)
  between operations  14.4 us (4%)
  loops' own time  4.07 us (1%)
    psum x1, waiting for transfers between devices, on_device(): lax.psum((weight_left, weight_right, gain_part, bias_part), ('row', 'col'))  121 us
    psum x1, waiting for transfers between devices, on_device(): lax.psum(right_acc.astype(jnp.bfloat16), 'row').astype(jnp.float32)  50.2 us
    reduce_scatter x1, waiting for transfers between devices, on_device(): lax.psum_scatter(projection_running_sum.astype(jnp.bfloat16), 'row', scat...  37.1 us
    all_gather x1, waiting for transfers between devices, on_device(): right_every = lax.all_gather(right_rows, 'row', axis=1, tiled=True)  21.7 us
    all_gather x1, blocking collectives, lax.all_gather(inner_x, along_axis).sum(axis=0)  19.8 us
    reduce_scatter x1, waiting for transfers between devices, on_device(): lax.psum_scatter(proj_partial, 'col', scatter_dimension=0, tiled=True)  18.8 us
    all_gather x1, blocking collectives, on_device(): lax.all_gather(right_local, 'col', axis=0, tiled=True)  18 us
    all_gather x1, blocking collectives, on_device(): lax.all_gather(left_local, 'col', axis=0, tiled=True)  16.3 us
  transfers between devices with their start and end apart: 6, of which 6 were waited for; matrix products, arithmetic and copies ran while one was open for 4% of the time, Pallas kernels for 0%

profile of v1, /device:TPU:0, one launch (start us, length us, event | category | flops | bytes accessed | tf_op | source)
XLA Modules:
  0.0 381.0 jit_solution(3695146156068478806)
XLA Ops:
  11.1 18.0 %all_gather.16 = bf16[128,16,32]{2,1,0:T(8,128)(2,1)} all-gather(bf16[32,16,32]{2,1,0:T(8,128)(2,1)S(1)} %bitcast.128), channel_id=1, replica_groups=mesh['row'=8,'col'=4] {'col'}, dimensions={0}, use_global_device_ids=true | all-gather | bytes 163840 | tf_op jit(solution)/shard_map/all_gather | solution.py:55
  29.6 16.3 %all_gather.15 = bf16[128,16,32]{2,1,0:T(8,128)(2,1)S(1)} all-gather(bf16[32,16,32]{2,1,0:T(8,128)(2,1)S(1)} %bitcast.129), channel_id=1, replica_groups=mesh['row'=8,'col'=4] {'col'}, dimensions={0}, use_global_device_ids=true | all-gather | bytes 163840 | tf_op jit(solution)/shard_map/all_gather | solution.py:54
  46.8 21.7 %all-gather.3.cloned.1.call-done = bf16[128,128,32]{2,1,0:T(8,128)(2,1)} async-done(((bf16[128,16,32]{2,1,0:T(8,128)(2,1)}), bf16[128,128,32]{2,1,0:T(8,128)(2,1)}) %all-gather.3.cloned.1.call-update) | async-done | bytes 1048592 | tf_op jit(solution)/shard_map/all_gather | solution.py:58
  69.8 1.8 copy.50
  71.6 32.6 %while.17 = (s32[]{:T(128)}, f32[128,32,32]{0,2,1:T(8,128)}, f32[1024,128]{1,0:T(8,128)S(1)}, bf16[2,8,32,128]{3,2,1,0:T(8,128)(2,1)}, bf16[2,128,8,32]{1,3,2,0:...) while((s32[]{:T(128)}, f32[128,32,32]{0,2,1:T(8,128)}, ...), condition=%wide.region_3.4_spmd.clone, body=%wide.region_2.3_spmd.clone.sunk | while | flops 404193280 | bytes 15928666 | solution.py:108
  74.8 1.7 fusion.79
  76.5 2.2 reshape.96
  81.1 1.6 reshape.95
  82.7 1.5 fusion.78
  85.3 2.1 fusion.81
  90.6 1.7 fusion.79
  92.3 2.2 reshape.96
  96.9 1.6 reshape.95
  98.5 2.6 fusion.78
  102.1 2.1 fusion.81
  104.3 1.8 convert_element_type.69
  106.1 1.5 convert_reduce_fusion.1
  107.6 2.1 copy.51
  109.9 50.2 %all-reduce.4.cloned.1.call-done = bf16[128,32,32]{0,2,1:T(8,128)(2,1)} async-done(((bf16[128,32,32]{0,2,1:T(8,128)(2,1)}), bf16[128,32,32]{0,2,1:T(8,128)(2,1)}) %all-reduce.4.cloned.1.call-update) | async-done | bytes 262160 | tf_op jit(solution)/shard_map/psum | solution.py:116
  161.0 19.8 %all-gather = bf16[512,16,32]{0,2,1:T(8,128)(2,1)S(1)} all-gather(bf16[128,16,32]{0,2,1:T(8,128)(2,1)S(1)} %fusion.28), channel_id=2, replica_groups=mesh['row'=8,'col'=4] {'col'}, dimensions={0}, use_global_device_ids=true | all-gather | bytes 655360 | tf_op jit(solution)/shard_map/all_gather | solution.py:6
  182.8 2.9 reduce-scatter.4.cloned.1.call-done
  190.8 120.9 %all-reduce.6.cloned.1.call-done = (f32[256,32]{0,1:T(8,128)}, f32[256,32]{0,1:T(8,128)}, f32[256]{0:T(256)}, f32[128]{0:T(128)}) async-done(((f32[256,32]{0,1:T(8,128)}, f32[256,32]{0,1:T(8,128)}, f32[256]{0:T(256)}, f32[128]{0:T(128)}), (f32[256,32]{0,1:T(8,128)}, f32[256,32]{0,1:T(8,128)}, f32[256]{0:T(256)}, f32[128]{0:T(128)})) %all-reduce.6.cloned.1.call-update) | async-done | bytes 67088 | tf_op jit(solution)/shard_map/psum | solution.py:157
  314.4 37.1 %reduce-scatter.6.cloned.1.call-done = bf16[128,128]{1,0:T(8,128)(2,1)} async-done(((bf16[1024,128]{1,0:T(8,128)(2,1)}), bf16[128,128]{1,0:T(8,128)(2,1)}) %reduce-scatter.6.cloned.1.call-update) | async-done | bytes 32784 | tf_op jit(solution)/shard_map/reduce_scatter | solution.py:158
  354.0 18.8 %reduce-scatter.8.cloned.1.call-done = f32[32,128]{1,0:T(8,128)} async-done(((f32[128,128]{1,0:T(8,128)}), f32[32,128]{1,0:T(8,128)}) %reduce-scatter.8.cloned.1.call-update) | async-done | bytes 16400 | tf_op jit(solution)/shard_map/reduce_scatter | solution.py:161
  (106 shorter events, 30.2 us)
Async XLA Ops:
  7.2 3.6 copy-start
  7.2 22.1 %copy-start.12 = (bf16[256,32]{0,1:T(8,128)(2,1)S(1)}, bf16[256,32]{0,1:T(8,128)(2,1)}, u32[]{:S(2)}) copy-start(bf16[256,32]{0,1:T(8,128)(2,1)} %param.11) | copy-start | bytes 49156
  7.2 61.3 %all-gather.3.cloned.1.call-start = ((), (), s32[]{:S(2)}) async-start(), calls=%async_computation.3 | async-start | bytes 4718592 | tf_op jit(solution)/shard_map/all_gather | solution.py:58
  8.3 2.4 copy-start.8
  10.8 18.8 %copy-start.5 = (bf16[32,16,256]{2,1,0:T(8,128)(2,1)}, bf16[32,16,256]{2,1,0:T(8,128)(2,1)S(1)}, u32[]{:S(2)}) copy-start(bf16[32,16,256]{2,1,0:T(8,128)(2,1)S(1)} %fusion.21) | copy-start | bytes 786436
  29.1 131.0 %all-reduce.4.cloned.1.call-start = ((), (), s32[]{:S(2)}) async-start(), calls=%async_computation.5 | async-start | bytes 524288 | tf_op jit(solution)/shard_map/psum | solution.py:116
  45.9 25.7 %copy-start.1 = (bf16[1024,128]{1,0:T(8,128)(2,1)S(1)}, bf16[1024,128]{1,0:T(8,128)(2,1)}, u32[]{:S(2)}) copy-start(bf16[1024,128]{1,0:T(8,128)(2,1)} %param.13) | copy-start | bytes 786436
  82.7 1.6 copy-start.15
  82.7 1.9 copy-start.16
  84.3 3.1 copy-start.3
  98.5 2.6 copy-start.15
  98.5 2.9 copy-start.16
  101.1 3.1 copy-start.3
  106.1 79.6 %reduce-scatter.4.cloned.1.call-start = ((), (), s32[]{:S(2)}) async-start(), calls=%async_computation.4 | async-start | bytes 655360 | tf_op jit(solution)/shard_map/reduce_scatter | solution.py:113
  107.6 74.3 %copy-start.6 = (bf16[32,16,256]{2,1,0:T(8,128)(2,1)S(1)}, bf16[32,16,256]{2,1,0:T(8,128)(2,1)}, u32[]{:S(2)}) copy-start(bf16[32,16,256]{2,1,0:T(8,128)(2,1)} %copy-done.5) | copy-start | bytes 786436
  109.8 75.9 %copy-start.13 = (bf16[256,32]{0,1:T(8,128)(2,1)S(1)}, bf16[256,32]{0,1:T(8,128)(2,1)}, u32[]{:S(2)}) copy-start(bf16[256,32]{0,1:T(8,128)(2,1)} %param.11) | copy-start | bytes 49156
  109.8 77.0 %copy-start.14 = (f32[256]{0:T(256)S(1)}, f32[256]{0:T(256)}, u32[]{:S(2)}) copy-start(f32[256]{0:T(256)} %param.10) | copy-start | bytes 3076
  109.8 201.9 %all-reduce.6.cloned.1.call-start = ((), (), s32[]{:S(2)}) async-start(), calls=%async_computation.8 | async-start | bytes 134144 | tf_op jit(solution)/shard_map/psum | solution.py:157
  180.8 6.3 %copy-start.4 = (bf16[32,16,256]{2,1,0:T(8,128)(2,1)S(1)}, bf16[32,16,256]{2,1,0:T(8,128)(2,1)}, u32[]{:S(2)}) copy-start(bf16[32,16,256]{2,1,0:T(8,128)(2,1)} %param.9) | copy-start | bytes 786436
  180.8 6.3 %copy-start.9 = (f32[32,16]{1,0:T(8,128)S(1)}, f32[32,16]{1,0:T(8,128)}, u32[]{:S(2)}) copy-start(f32[32,16]{1,0:T(8,128)} %copy-done.8) | copy-start | bytes 6148
  180.8 6.3 %copy-start.11 = (f32[32,16]{1,0:T(8,128)S(1)}, f32[32,16]{1,0:T(8,128)}, u32[]{:S(2)}) copy-start(f32[32,16]{1,0:T(8,128)} %copy-done.10) | copy-start | bytes 6148
  185.6 2.3 copy-start.7
  188.8 162.7 %reduce-scatter.6.cloned.1.call-start = ((), (), s32[]{:S(2)}) async-start(), calls=%async_computation.6 | async-start | bytes 294912 | tf_op jit(solution)/shard_map/reduce_scatter | solution.py:158
  189.6 183.3 %reduce-scatter.8.cloned.1.call-start = ((), (), s32[]{:S(2)}) async-start(), calls=%async_computation.7 | async-start | bytes 81920 | tf_op jit(solution)/shard_map/reduce_scatter | solution.py:161
  (5 other events, 4.1 us)
Sparse Core Ops, SparseCore 0:
  29.3 39.2 all-gather.2
  106.2 53.8 all-reduce.3
  162.4 23.2 reduce-scatter.3
  192.2 119.4 all-reduce.5
  314.6 36.8 reduce-scatter.5
  353.5 19.2 reduce-scatter.7
